TPU v7x, 32 devices: a whole 2x2x4 slice. The times are simulated.
32 devices in a mesh: expert: 8 (over y, x, core), hidden: 4 (over z).
Axes of the slice: x: 2, y: 2, z: 4, core: 2. Of those that a mesh axis runs over, the one named last changes fastest.
Arguments:
- weight: bfloat16 [8, 1536, 4096], P('expert', 'hidden'), may hold values from -0.15625 to 0.15625
- scales: float32 [8, 12, 32], P('expert'), may hold values from 0.5 to 2
- act_own: bfloat16 [8, 128, 1536], P('expert', None, 'hidden'), may hold values from -6 to 6
- dy_own: bfloat16 [8, 128, 4096], P('expert'), may hold values from -6 to 6
- own_count: int32 [8], P('expert'), may hold values from 1 to 128, as said below
- act_help: bfloat16 [8, 32, 1536], P('expert', None, 'hidden'), may hold values from -6 to 6
- dy_help: bfloat16 [8, 32, 4096], P('expert'), may hold values from -6 to 6
- help_count: int32 [8], P('expert'), may hold values from 1 to 32, as said below
- hot: int32 [1], replicated, may hold values from 0 to 7
Outputs:
- y_own: bfloat16 [8, 128, 4096], P('expert', None, 'hidden')
- dact_own: bfloat16 [8, 128, 1536], P('expert', None, 'hidden')
- own_grad: bfloat16 [8, 1536, 4096], P('expert', 'hidden')
- y_help: bfloat16 [8, 32, 4096], P('expert', None, 'hidden')
- dact_help: bfloat16 [8, 32, 1536], P('expert', None, 'hidden')
- hot_grad: float32 [1536, 4096], P('hidden', 'expert')
Inputs may be any that keep to these rules, and one draw needn't show every extreme that they name: `own_count`: some expert has exactly 128 live rows. `help_count`: some group has exactly 32 live rows.
All inputs are finite; a program needn't handle non-finite values.
Results may differ from a plain program's by a relative error of at most 0.013.
Values may be sent and summed in bfloat16 or wider, within the bound.
No kernel may reach another device: no remote copies, remote signals or barrier semaphores. Data moves between devices by JAX's collectives and lax.ppermute only.
A program may use at most 64 MiB of HBM per device.

v0:
```python
import jax
import jax.numpy as jnp
from jax import lax
from jax.sharding import PartitionSpec as P

block_edge = 128


def from_root(block, axis, source):
    block = jnp.where(lax.axis_index(axis) == source, block, jnp.zeros_like(block))
    return lax.psum(block, axis)


def dequant(weight, scales, slice_start):
    height = weight.shape[1]
    depth = weight.shape[2]
    blocks = (slice_start + jnp.arange(height, dtype=jnp.int32)) // block_edge
    select = (blocks[:, None] == jnp.arange(scales.shape[1], dtype=jnp.int32)[None, :]).astype(
        jnp.float32
    )
    row_scale = jnp.einsum("fb,ebc->efc", select, scales, precision=lax.Precision.HIGHEST)
    shaped = weight.reshape(weight.shape[0], height, depth // block_edge, block_edge).astype(
        jnp.float32
    )
    shaped = shaped * row_scale[..., None]
    return shaped.reshape(weight.shape).astype(jnp.bfloat16)


def masked(values, count):
    live = jnp.arange(values.shape[1], dtype=jnp.int32)[None, :, None] < count[:, None, None]
    return jnp.where(live, values, jnp.zeros_like(values))


def body(weight, scales, act_own, dy_own, own_count, act_help, dy_help, help_count, hot):
    slice_start = lax.axis_index("hidden") * weight.shape[1]
    own_weight = dequant(weight, scales, slice_start)
    experts_here = weight.shape[0]
    hot_index = hot[0]
    hot_local = hot_index % experts_here
    hot_root = hot_index // experts_here
    own_rows = masked(act_own, own_count)
    own_grads = masked(dy_own, own_count)
    help_rows = masked(act_help, help_count)[0]
    help_grads = masked(dy_help, help_count)[0]
    partial_value = jnp.einsum(
        "erf,efd->erd", own_rows, own_weight, preferred_element_type=jnp.float32
    )
    dact = jnp.einsum("erd,efd->erf", own_grads, own_weight, preferred_element_type=jnp.float32)
    gradient = jnp.einsum("erf,erd->efd", own_rows, own_grads, preferred_element_type=jnp.float32)
    dact_own = dact.astype(jnp.bfloat16)
    own_grad = gradient.astype(jnp.bfloat16)
    chosen = lax.dynamic_index_in_dim(own_weight, hot_local, 0, keepdims=False)
    hot_weight = from_root(chosen, "expert", hot_root)
    help_partial_value = jnp.dot(help_rows, hot_weight, preferred_element_type=jnp.float32)
    dact = lax.dot_general(
        help_grads, hot_weight, (((1,), (1,)), ((), ())), preferred_element_type=jnp.float32
    )
    gradient = lax.dot_general(
        help_rows, help_grads, (((0,), (0,)), ((), ())), preferred_element_type=jnp.float32
    )
    summed = lax.psum_scatter(gradient, "expert", scatter_dimension=1, tiled=True)
    help_partial = help_partial_value[None]
    dact_help = dact.astype(jnp.bfloat16)[None]
    y_own, y_help = (
        lax.psum_scatter(
            partial_value.astype(jnp.bfloat16), "hidden", scatter_dimension=2, tiled=True
        ).astype(jnp.float32),
        lax.psum_scatter(
            help_partial.astype(jnp.bfloat16), "hidden", scatter_dimension=2, tiled=True
        ).astype(jnp.float32),
    )
    return (
        y_own.astype(jnp.bfloat16),
        dact_own,
        own_grad,
        y_help.astype(jnp.bfloat16),
        dact_help,
        summed,
    )


def solution(mesh):
    return jax.shard_map(
        body,
        mesh=mesh,
        in_specs=(
            P("expert", "hidden", None),
            P("expert", None, None),
            P("expert", None, "hidden"),
            P("expert", None, None),
            P("expert"),
            P("expert", None, "hidden"),
            P("expert", None, None),
            P("expert"),
            P(),
        ),
        out_specs=(
            P("expert", None, "hidden"),
            P("expert", None, "hidden"),
            P("expert", "hidden", None),
            P("expert", None, "hidden"),
            P("expert", None, "hidden"),
            P("hidden", "expert"),
        ),
        check_vma=False,
    )
```

profile of v0, /device:TPU:0, one launch (start us, length us, event | category | flops | bytes accessed | tf_op | source)
XLA Modules:
  0.0 194.3 jit_solution(13138229122066029622)
XLA Ops:
  8.0 0.0 all-reduce.2.cloned.1.call-start
  8.1 1.0 fusion.11
  9.1 3.8 %mul.18 = f32[384,32,128]{2,1,0:T(8,128)} broadcast(f32[384,32]{1,0:T(8,128)S(1)} %fusion.11), dimensions={0,1} | broadcast | bytes 6340608 | tf_op jit(solution)/shard_map/mul | solution.py:25
  12.9 7.2 %mul.19 = f32[1,384,4096]{2,1,0:T(8,128)} reshape(f32[384,32,128]{2,1,0:T(8,128)} %mul.18) | data formatting | bytes 12582912 | tf_op jit(solution)/shard_map/mul | solution.py:25
  20.7 6.8 %broadcast_select_fusion = (bf16[384,4096]{1,0:T(8,128)(2,1)}, bf16[384,4096]{1,0:T(8,128)(2,1)S(1)}) fusion(pred[]{:T(512)S(6)} %eq.21, f32[1,384,4096]{2,1,0:T(8,128)} %mul.19, bf16[1,384,4096]{2,1,0:T(8,128)(2,1)} %param.9), kind=kLoop, calls=%fused_computation.8 | loop fusion | flops 6291456 | bytes 15728641 | tf_op jit(solution)/shard_map/jit(_where)/select_n | solution.py:10
  27.5 0.0 copy-start.3
  27.5 0.0 all-reduce.2.cloned.1.call-update
  27.6 0.0 copy-start.4
  27.6 0.0 reduce-scatter.4.cloned.1.call-start
  28.3 0.1 copy-done.3
  28.4 1.7 fusion.1
  30.1 0.0 copy-start.2
  30.1 0.0 reduce-scatter.4.cloned.1.call-update
  30.2 0.0 reduce-scatter.6.cloned.1.call-start
  30.9 68.8 %all-reduce.2.cloned.1.call-done = bf16[384,4096]{1,0:T(8,128)(2,1)} async-done(((bf16[384,4096]{1,0:T(8,128)(2,1)}), bf16[384,4096]{1,0:T(8,128)(2,1)}) %all-reduce.2.cloned.1.call-update) | async-done | bytes 3145744 | tf_op jit(solution)/shard_map/psum | solution.py:11
  99.7 0.0 copy-done.4
  99.7 3.3 %fusion.2 = bf16[1,32,4096]{2,1,0:T(8,128)(2,1)} fusion(bf16[384,4096]{1,0:T(8,128)(2,1)} %all-reduce.2.cloned.1.call-done, bf16[1,32,384]{2,1,0:T(8,128)(2,1)S(1)} %copy-done.4, pred[32]{0:T(512)(128)(4,1)S(1)} %iota_compare_fusion.2), kind=kOutput, calls=%fused_computation.6 | convolution fusion | flops 100806656 | bytes 3432480 | tf_op jit(solution)/shard_map/dot_general | solution.py:54
  103.0 0.0 reduce-scatter.6.cloned.1.call-update
  103.1 0.0 reduce-scatter.8.cloned.1.call-start
  103.1 0.0 copy-done.2
  103.1 3.7 %fusion.8 = f32[384,4096]{1,0:T(8,128)} fusion(bf16[1,32,4096]{2,1,0:T(8,128)(2,1)S(1)} %copy-done.2, pred[32]{0:T(512)(128)(4,1)S(1)} %iota_compare_fusion.2, bf16[1,32,384]{2,1,0:T(8,128)(2,1)S(1)} %copy-done.4), kind=kOutput, calls=%fused_computation.16 | convolution fusion | flops 100806656 | bytes 6578208 | tf_op jit(solution)/shard_map/dot_general | solution.py:58
  106.8 0.0 reduce-scatter.8.cloned.1.call-update
  106.9 0.0 copy-start.1
  106.9 4.1 %fusion = bf16[1,384,4096]{2,1,0:T(8,128)(2,1)} fusion(bf16[1,128,4096]{2,1,0:T(8,128)(2,1)} %param.12, pred[128]{0:T(512)(128)(4,1)S(1)} %iota_compare_fusion.3, bf16[1,128,384]{2,1,0:T(8,128)(2,1)S(1)} %copy-done.3), kind=kOutput, calls=%fused_computation.2 | convolution fusion | flops 404799488 | bytes 4292736 | tf_op jit(solution)/shard_map/erf,erd->efd/dot_general | solution.py:49
  110.9 0.0 copy-done.1
  110.9 0.0 copy-start
  110.9 1.7 fusion.4
  112.7 0.2 copy-done
  112.8 1.7 fusion.5
  114.5 0.0 reduce-scatter.4.cloned.1.call-done
  114.5 8.7 %reduce-scatter.6.cloned.1.call-done = bf16[1,32,1024]{2,1,0:T(8,128)(2,1)} async-done(((bf16[1,32,4096]{2,1,0:T(8,128)(2,1)}), bf16[1,32,1024]{2,1,0:T(8,128)(2,1)}) %reduce-scatter.6.cloned.1.call-update) | async-done | bytes 65552 | tf_op jit(solution)/shard_map/reduce_scatter | solution.py:68
  123.2 63.6 %reduce-scatter.8.cloned.1.call-done = f32[384,512]{1,0:T(8,128)} async-done(((f32[384,4096]{1,0:T(8,128)}), f32[384,512]{1,0:T(8,128)}) %reduce-scatter.8.cloned.1.call-update) | async-done | bytes 786448 | tf_op jit(solution)/shard_map/reduce_scatter | solution.py:61
  (3 shorter events, 0.0 us)
Async XLA Ops:
  8.0 91.7 %all-reduce.2.cloned.1.call-start = ((), (), s32[]{:S(2)}) async-start(), calls=%async_computation.4 | async-start | bytes 6291456 | tf_op jit(solution)/shard_map/psum | solution.py:11
  27.5 0.9 copy-start.3
  27.6 72.2 %copy-start.4 = (bf16[1,32,384]{2,1,0:T(8,128)(2,1)S(1)}, bf16[1,32,384]{2,1,0:T(8,128)(2,1)}, u32[]{:S(2)}) copy-start(bf16[1,32,384]{2,1,0:T(8,128)(2,1)} %param.14) | copy-start | bytes 73732
  27.6 86.9 %reduce-scatter.4.cloned.1.call-start = ((), (), s32[]{:S(2)}) async-start(), calls=%async_computation.3 | async-start | bytes 1310720 | tf_op jit(solution)/shard_map/reduce_scatter | solution.py:65
  30.1 73.0 %copy-start.2 = (bf16[1,32,4096]{2,1,0:T(8,128)(2,1)S(1)}, bf16[1,32,4096]{2,1,0:T(8,128)(2,1)}, u32[]{:S(2)}) copy-start(bf16[1,32,4096]{2,1,0:T(8,128)(2,1)} %param.15) | copy-start | bytes 786436
  30.2 93.0 %reduce-scatter.6.cloned.1.call-start = ((), (), s32[]{:S(2)}) async-start(), calls=%async_computation.5 | async-start | bytes 327680 | tf_op jit(solution)/shard_map/reduce_scatter | solution.py:68
  103.1 83.7 %reduce-scatter.8.cloned.1.call-start = ((), (), s32[]{:S(2)}) async-start(), calls=%async_computation.6 | async-start | bytes 7077888 | tf_op jit(solution)/shard_map/reduce_scatter | solution.py:61
  106.9 4.1 %copy-start.1 = (bf16[1,128,4096]{2,1,0:T(8,128)(2,1)S(1)}, bf16[1,128,4096]{2,1,0:T(8,128)(2,1)}, u32[]{:S(2)}) copy-start(bf16[1,128,4096]{2,1,0:T(8,128)(2,1)} %param.12) | copy-start | bytes 3145732
  110.9 1.9 copy-start
Sparse Core Ops, SparseCore 0:
  27.7 72.0 all-reduce.1
Sparse Core Ops, SparseCore 1:
  30.9 29.9 reduce-scatter.3
  103.1 20.0 reduce-scatter.5
  127.0 59.7 reduce-scatter.7
where the time goes:
time: 195 us; the launch traced here: 194 us
  waiting for transfers between devices  141 us (72%)
  between operations  17.7 us (9%)
  matrix products  17.2 us (9%)
  local copies, waits for them, and re-layouts  11.3 us (6%)
  other arithmetic  6.87 us (4%)
    psum x1, waiting for transfers between devices, from_root(): return lax.psum(block, axis)  68.8 us
    reduce_scatter x1, waiting for transfers between devices, body(): lax.psum_scatter(gradient, 'expert', scatter_dimension=1, tiled=True)  63.6 us
    mul x2, local copies, waits for them, and re-layouts, dequant(): shaped = shaped * row_scale[..., None]  11 us
    reduce_scatter x1, waiting for transfers between devices, body(): lax.psum_scatter(help_partial.astype(jnp.bfloat16), 'hidden', scatter_dim...  8.65 us
    select_n x1, other arithmetic, from_root(): jnp.where(lax.axis_index(axis) == source, block, jnp.zeros_like(block))  6.85 us
    dot_general x1, matrix products, body(): jnp.einsum('erf,erd->efd', own_rows, own_grads, preferred_element_type=jn...  4.06 us
  transfers between devices with their start and end apart: 4, of which 3 were waited for; matrix products, arithmetic and copies ran while one was open for 8% of the time, Pallas kernels for 0%

commit v1 on v0

--- a/solution.py
+++ b/solution.py
@@ -1,7 +1,12 @@
+import functools
+
 import jax
 import jax.numpy as jnp
 from jax import lax
+from jax.experimental import pallas as pl
+from jax.experimental.pallas import tpu as pltpu
 from jax.sharding import PartitionSpec as P
+
 
 block_edge = 128
 
@@ -31,7 +36,7 @@
     return jnp.where(live, values, jnp.zeros_like(values))
 
 
-def body(weight, scales, act_own, dy_own, own_count, act_help, dy_help, help_count, hot):
+def weights_to_rows(weight, scales, act_own, dy_own, own_count, act_help, dy_help, help_count, hot):
     slice_start = lax.axis_index("hidden") * weight.shape[1]
     own_weight = dequant(weight, scales, slice_start)
     experts_here = weight.shape[0]
@@ -79,7 +84,283 @@
     )
 
 
+by_weight = (((1,), (1,)), ((), ()))
+by_row = (((0,), (0,)), ((), ()))
+
+
+def product(left, right, dims=(((1,), (0,)), ((), ()))):
+    return lax.dot_general(left, right, dims, preferred_element_type=jnp.float32)
+
+
+def live_rows(values, count):
+    live = lax.broadcasted_iota(jnp.int32, values.shape, 0) < count
+    return jnp.where(live, values, jnp.zeros_like(values))
+
+
+def scale_into(stored, weight_ref, scale_of, first):
+    height, width = weight_ref.shape
+    for column in range(width // block_edge):
+        cols = slice(column * block_edge, (column + 1) * block_edge)
+        for row in range(height // block_edge):
+            part = slice(row * block_edge, (row + 1) * block_edge)
+            stored[part, cols] = (
+                weight_ref[part, cols].astype(jnp.float32) * scale_of(row, first + column)
+            ).astype(jnp.bfloat16)
+
+
+def pick_into(stored, mine, own_ref, other_ref, scale_of, first):
+    height, width = own_ref.shape
+    for column in range(width // block_edge):
+        cols = slice(column * block_edge, (column + 1) * block_edge)
+        for row in range(height // block_edge):
+            part = slice(row * block_edge, (row + 1) * block_edge)
+            block = jnp.where(mine, own_ref[part, cols], other_ref[part, cols])
+            stored[part, cols] = (
+                block.astype(jnp.float32) * scale_of(row, first + column)
+            ).astype(jnp.bfloat16)
+
+
+hbm_place = pl.BlockSpec(memory_space=pltpu.HBM)
+smem_place = pl.BlockSpec(memory_space=pltpu.SMEM)
+vmem_place = pl.BlockSpec(memory_space=pltpu.VMEM)
+grant = pltpu.CompilerParams(vmem_limit_bytes=16 * 2**20)
+
+
+def own_forward_kernel(pieces, scale_ref, count_ref, rows_ref, weight_ref, *refs):
+    out_refs = refs[:pieces]
+    (stored,) = refs[pieces:]
+    height, depth = weight_ref.shape
+    width = depth // pieces
+    place = lax.axis_index("hidden")
+    top = place * (height // block_edge)
+    live = live_rows(rows_ref[...], count_ref[0])
+    for i in range(pieces):
+        start = pl.multiple_of((place ^ i) * width, width)
+        block = weight_ref.at[:, pl.ds(start, width)]
+        first = start // block_edge
+        scale_into(stored.at[i % 2], block, lambda r, c: scale_ref[top + r, 0, c], first)
+        out_refs[i][...] = product(live, stored[i % 2]).astype(jnp.bfloat16)
+
+
+def own_forward(scales, weight, rows, count, pieces):
+    height, depth = weight.shape
+    nrows = rows.shape[0]
+    width = depth // pieces
+    return pl.pallas_call(
+        functools.partial(own_forward_kernel, pieces),
+        in_specs=[smem_place] * 2 + [vmem_place] * 2,
+        out_specs=[vmem_place] * pieces,
+        out_shape=[jax.ShapeDtypeStruct((nrows, width), jnp.bfloat16)] * pieces,
+        scratch_shapes=[pltpu.VMEM((2, height, width), jnp.bfloat16)],
+        compiler_params=grant,
+        cost_estimate=pl.CostEstimate(
+            flops=2 * nrows * height * depth,
+            bytes_accessed=2 * height * depth + 2 * nrows * (height + depth),
+            transcendentals=0,
+        ),
+        name="own_forward",
+    )(scales, count, rows, weight)
+
+
+def own_backward_kernel(scale_ref, count_ref, rows_ref, grads_ref, weight_ref, ours, theirs,
+                        dact_ref, grad_ref, hot_ref, stored, made, dact, total, hot, out_sems, end_sems):
+    height, _ = weight_ref.shape
+    steps, _, width = made.shape
+    top = lax.axis_index("hidden") * (height // block_edge)
+    live = live_rows(rows_ref[...], count_ref[0])
+    out = []
+    for i in range(steps):
+        cols = slice(i * width, (i + 1) * width)
+        live_grads = live_rows(grads_ref[:, cols], count_ref[0])
+        made[i] = product(live, live_grads, by_row).astype(jnp.bfloat16)
+        out.append(pltpu.make_async_copy(made.at[i], grad_ref.at[:, cols], out_sems.at[i]))
+        out[-1].start()
+        first = i * (width // block_edge)
+        scale_into(stored.at[i % 2], weight_ref.at[:, cols], lambda r, c: scale_ref[top + r, 0, c], first)
+        part = product(live_grads, stored[i % 2], by_weight)
+        total[...] = part if i == 0 else total[...] + part
+    dact[...] = total[...].astype(jnp.bfloat16)
+    out.append(pltpu.make_async_copy(dact, dact_ref, end_sems.at[0]))
+    out[-1].start()
+    hot[...] = product(ours[:, :height], ours[:, height:], by_row) + product(
+        theirs[:, :height], theirs[:, height:], by_row
+    )
+    out.append(pltpu.make_async_copy(hot, hot_ref, end_sems.at[1]))
+    out[-1].start()
+    for copy in out:
+        copy.wait()
+
+
+def own_backward(scales, weight, rows, grads, count, ours, theirs):
+    height, depth = weight.shape
+    nrows = rows.shape[0]
+    hrows, wide = ours.shape[0], ours.shape[1] - height
+    width = 1024
+    steps = depth // width
+    return pl.pallas_call(
+        own_backward_kernel,
+        in_specs=[smem_place] * 2 + [vmem_place] * 5,
+        out_specs=[hbm_place] * 3,
+        out_shape=[
+            jax.ShapeDtypeStruct((nrows, height), jnp.bfloat16),
+            jax.ShapeDtypeStruct((height, depth), jnp.bfloat16),
+            jax.ShapeDtypeStruct((height, wide), jnp.float32),
+        ],
+        scratch_shapes=[
+            pltpu.VMEM((2, height, width), jnp.bfloat16),
+            pltpu.VMEM((steps, height, width), jnp.bfloat16),
+            pltpu.VMEM((nrows, height), jnp.bfloat16),
+            pltpu.VMEM((nrows, height), jnp.float32),
+            pltpu.VMEM((height, wide), jnp.float32),
+            pltpu.SemaphoreType.DMA((steps,)),
+            pltpu.SemaphoreType.DMA((2,)),
+        ],
+        compiler_params=grant,
+        cost_estimate=pl.CostEstimate(
+            flops=4 * nrows * height * depth + 4 * hrows * height * wide,
+            bytes_accessed=4 * height * depth + 4 * nrows * (height + depth) + 4 * height * wide,
+            transcendentals=0,
+        ),
+        name="own_backward",
+    )(scales, count, rows, grads, weight, ours, theirs)
+
+
+def help_kernel(count, pieces, wide, hot_ref, scale_ref, other_scale_ref, own_ref, other_ref, *refs):
+    in_refs, out_refs = refs[:count], refs[count : 2 * count]
+    ours_ref, theirs_ref = refs[2 * count : 2 * count + 2]
+    stored, total = refs[2 * count + 2 :]
+    height, depth = own_ref.shape
+    width = depth // pieces
+    me, place = lax.axis_index("expert"), lax.axis_index("hidden")
+    mine = me % 2 == hot_ref[0] % 2
+    top = place * (height // block_edge)
+    each = in_refs[0].shape[0]
+    starts = [pl.multiple_of((place ^ piece) * width, width) for piece in range(pieces)]
+
+    def rows(cols):
+        return jnp.concatenate([ref[:, cols] for ref in in_refs], axis=0)
+
+    def scale_of(row, column):
+        return jnp.where(mine, scale_ref[top + row, 0, column], other_scale_ref[top + row, 0, column])
+
+    acts = rows(slice(0, height))
+    for ref, index in ((ours_ref, me), (theirs_ref, me ^ 1)):
+        ref[:, :height] = acts
+        ref[:, height:] = rows(pl.ds(pl.multiple_of(height + index * wide, block_edge), wide))
+    for i in range(pieces):
+        first = starts[i] // block_edge
+        spot = stored.at[i % 2]
+        cols = pl.ds(starts[i], width)
+        pick_into(spot, mine, own_ref.at[:, cols], other_ref.at[:, cols], scale_of, first)
+        value = product(acts, spot[...]).astype(jnp.bfloat16)
+        for k, ref in enumerate(out_refs):
+            ref[:, i * width : (i + 1) * width] = value[k * each : (k + 1) * each]
+        grads = rows(pl.ds(pl.multiple_of(height + starts[i], block_edge), width))
+        part = product(grads, spot[...], by_weight)
+        total[...] = part if i == 0 else total[...] + part
+    for k, ref in enumerate(out_refs):
+        ref[:, depth:] = total[k * each : (k + 1) * each, :].astype(jnp.bfloat16)
+
+
+def help_both(hot, scales, other_scales, weight, other_weight, rows, pieces, wide):
+    height, depth = weight.shape
+    count, each = len(rows), rows[0].shape[0]
+    nrows = count * each
+    width = depth // pieces
+    shape = lambda r, c: jax.ShapeDtypeStruct((r, c), jnp.bfloat16)
+    return pl.pallas_call(
+        functools.partial(help_kernel, count, pieces, wide),
+        in_specs=[smem_place] * 3 + [vmem_place] * (2 + count),
+        out_specs=[vmem_place] * (count + 2),
+        out_shape=[shape(each, depth + height)] * count + [shape(nrows, height + wide)] * 2,
+        scratch_shapes=[
+            pltpu.VMEM((2, height, width), jnp.bfloat16),
+            pltpu.VMEM((nrows, height), jnp.float32),
+        ],
+        compiler_params=grant,
+        cost_estimate=pl.CostEstimate(
+            flops=4 * nrows * height * depth,
+            bytes_accessed=2 * height * depth + 4 * nrows * (height + depth),
+            transcendentals=0,
+        ),
+        name="help_both",
+    )(hot, scales, other_scales, weight, other_weight, *rows)
+
+
+def swap(block, axis, size, mask):
+    return lax.ppermute(block, axis, [(i, i ^ mask) for i in range(size)])
+
+
+def over_hidden(pieces, size):
+    return [pieces[0]] + [swap(pieces[k], "hidden", size, k) for k in range(1, size)]
+
+
+def add_up(parts):
+    total = parts[0].astype(jnp.float32)
+    for part in parts[1:]:
+        total = total + part.astype(jnp.float32)
+    return total.astype(jnp.bfloat16)
+
+
+def pick(options, index):
+    chosen = options[0]
+    for k in range(1, len(options)):
+        chosen = jnp.where(index == k, options[k], chosen)
+    return chosen
+
+
+def rows_to_owner(
+    groups, slices, weight, scales, act_own, dy_own, own_count, act_help, dy_help, help_count, hot
+):
+    _, depth = weight.shape[1:]
+    chips = groups // 2
+    me = lax.axis_index("expert").astype(jnp.int32)
+    away = (hot[0] // 2) ^ (me // 2)
+    scales = jnp.transpose(scales, (1, 0, 2))
+    other_scales = swap(scales, "expert", groups, 1)
+    other_weight = swap(weight[0], "expert", groups, 1)
+
+    def over_chips(parts):
+        return [parts[0]] + [swap(parts[k], "expert", groups, 2 * k) for k in range(1, chips)]
+
+    joined = jnp.concatenate([act_help, dy_help], axis=2)
+    rows = over_chips([masked(joined, help_count)[0]] * chips)
+    own_parts = over_hidden(own_forward(scales, weight[0], act_own[0], own_count, slices), slices)
+
+    wide = depth // groups
+    *results, ours, theirs = help_both(
+        hot, scales, other_scales, weight[0], other_weight, rows, slices, wide
+    )
+    theirs = swap(theirs, "expert", groups, 1)
+    result = pick(over_chips(results), away)
+    width = depth // slices
+    help_parts = over_hidden(
+        [result[:, k * width : (k + 1) * width] for k in range(slices)], slices
+    )
+    y_help = add_up(help_parts)
+    own_parts, _ = lax.optimization_barrier((own_parts, result))
+    y_own = add_up(own_parts)
+    dact_help = result[:, depth:]
+
+    dact_own, own_grad, hot_grad = own_backward(
+        scales, weight[0], act_own[0], dy_own[0], own_count, ours, theirs
+    )
+    return y_own[None], dact_own[None], own_grad[None], y_help[None], dact_help[None], hot_grad
+
+
 def solution(mesh):
+    groups, slices = mesh.shape["expert"], mesh.shape["hidden"]
+
+    def body(weight, scales, act_own, dy_own, own_count, act_help, dy_help, help_count, hot):
+        args = (weight, scales, act_own, dy_own, own_count, act_help, dy_help, help_count, hot)
+        experts, height, depth = weight.shape
+        few = groups * act_help.shape[1] <= 2 * height and groups in (2, 4, 8, 16)
+        even = height % block_edge == 0 and depth % 1024 == 0
+        even = even and depth % (groups * block_edge) == 0 and depth % (slices * 256) == 0
+        if experts == 1 and few and even and slices in (2, 4, 8):
+            return rows_to_owner(groups, slices, *args)
+        return weights_to_rows(*args)
+
     return jax.shard_map(
         body,
         mesh=mesh,

time: 195 us -> 68.4 us (0.35)
  waiting for transfers between devices: 141 us -> 25.4 us
  matrix products: 17.2 us -> 0 us
  starting transfers between devices: 0.17 us -> 17.1 us
  between operations: 17.7 us -> 2.69 us
  Pallas kernels: 0 us -> 10.8 us
  local copies, waits for them, and re-layouts: 11.3 us -> 7.51 us
  other arithmetic: 6.87 us -> 4.59 us
    reduce_scatter x3 -> x0, waiting for transfers between devices: 72.2 us -> none  [the longest x1 63.6 us: body(): lax.psum_scatter(gradient, 'expert', scatter_dimension=1, tiled=True)]
    psum x1 -> x0, waiting for transfers between devices: 68.8 us -> none  [from_root(): return lax.psum(block, axis)]
    ppermute x0 -> x15, waiting for transfers between devices: none -> 25.4 us  [swap(): return lax.ppermute(block, axis, [(i, i ^ mask) for i in range(size)])]
    dot_general x7 -> x0, matrix products: 17.2 us -> none  [the longest x1 4.06 us: body(): jnp.einsum('erf,erd->efd', own_rows, own_grads, preferred_element_type=jn...]
    ppermute x0 -> x15, starting transfers between devices: none -> 17.1 us  [swap(): return lax.ppermute(block, axis, [(i, i ^ mask) for i in range(size)])]
    mul x2 -> x0, local copies, waits for them, and re-layouts: 11 us -> none  [dequant(): shaped = shaped * row_scale[..., None]]
    pallas_call x0 -> x3, Pallas kernels: none -> 10.8 us  [the longest x1 4.36 us: own_backward(): pl.pallas_call(own_backward_kernel, in_specs=[smem_place] * 2 + [vmem_pla...]
    unnamed x10 -> x26, local copies, waits for them, and re-layouts: 0.34 us -> 6.89 us
  transfers between devices with their start and end apart: 4 -> 15, of which waited for: 3 -> 6; matrix products, arithmetic and copies ran while one was open for 8% -> 7% of each run, Pallas kernels for 0% -> 10%
where the time goes in v1:
time: 68.4 us; the launch traced here: 68 us
  waiting for transfers between devices  25.4 us (37%)
  starting transfers between devices  17.1 us (25%)
  Pallas kernels  10.8 us (16%)
  local copies, waits for them, and re-layouts  7.51 us (11%)
  other arithmetic  4.59 us (7%)
  between operations  2.69 us (4%)
    ppermute x15, waiting for transfers between devices, swap(): return lax.ppermute(block, axis, [(i, i ^ mask) for i in range(size)])  25.4 us
    ppermute x15, starting transfers between devices, swap(): return lax.ppermute(block, axis, [(i, i ^ mask) for i in range(size)])  17.1 us
    unnamed x26, local copies, waits for them, and re-layouts  6.89 us
    pallas_call x1, Pallas kernels, own_backward(): pl.pallas_call(own_backward_kernel, in_specs=[smem_place] * 2 + [vmem_pla...  4.36 us
    pallas_call x1, Pallas kernels, help_both(): pl.pallas_call(functools.partial(help_kernel, count, pieces, wide), in_sp...  3.84 us
    pallas_call x1, Pallas kernels, own_forward(): pl.pallas_call(functools.partial(own_forward_kernel, pieces), in_specs=[s...  2.55 us
    broadcast_in_dim x1, other arithmetic, rows_to_owner(): y_own[None]  1.82 us
  transfers between devices with their start and end apart: 15, of which 6 were waited for; matrix products, arithmetic and copies ran while one was open for 7% of the time, Pallas kernels for 10%

profile of v1, /device:TPU:0, one launch (start us, length us, event | category | flops | bytes accessed | tf_op | source)
XLA Modules:
  0.0 68.0 jit_solution(9868822887961075374)
XLA Ops:
  0.6 0.6 collective-permute-start.4
  1.9 1.1 %maximum_select_fusion.refs_0_ = bf16[32,4480]{1,0:T(8,128)(2,1)S(1)} fusion(bf16[32,4096]{1,0:T(8,128)(2,1)} %bitcast.32, bf16[32,384]{1,0:T(8,128)(2,1)} %bitcast.33, pred[32]{0:T(512)(128)(4,1)S(1)} %iota_compare_fusion), kind=kLoop, calls=%fused_computation.1 | loop fusion | flops 716800 | bytes 573472 | tf_op jit(solution)/shard_map/jit(_where)/select_n | solution.py:36
  2.9 2.5 %collective-permute-start.5 = (bf16[32,4480]{1,0:T(8,128)(2,1)S(1)}, bf16[32,4480]{1,0:T(8,128)(2,1)S(1)}, u32[]{:S(2)}, u32[]{:S(2)}) collective-permute-start(bf16[32,4480]{1,0:T(8,128)(2,1)S(1)} %maximum_select_fusion.refs_0_), channel_id=1, source_target_pairs={{0,8},{4,12},{8,0},{12,4},{16,24},{20,28},{24,16},{28,20},{1,9},{5... | collective-permute-start | bytes 860168 | tf_op jit(solution)/shard_map/ppermute | solution.py:291
  5.5 1.5 %collective-permute-start.6 = (bf16[32,4480]{1,0:T(8,128)(2,1)S(1)}, bf16[32,4480]{1,0:T(8,128)(2,1)S(1)}, u32[]{:S(2)}, u32[]{:S(2)}) collective-permute-start(bf16[32,4480]{1,0:T(8,128)(2,1)S(1)} %maximum_select_fusion.refs_0_), channel_id=1, source_target_pairs={{0,16},{4,20},{8,24},{12,28},{16,0},{20,4},{24,8},{28,12},{1,17},{... | collective-permute-start | bytes 860168 | tf_op jit(solution)/shard_map/ppermute | solution.py:291
  7.7 0.7 %collective-permute-done.3.other_scale_ref = f32[12,1,32]{2,1,0:T(1,128)S(1)} collective-permute-done((f32[12,1,32]{2,1,0:T(1,128)}, f32[12,1,32]{2,1,0:T(1,128)S(1)}, u32[]{:S(2)}, u32[]{:S(2)}) %collective-permute-start.3) | collective-permute-done | bytes 1568 | tf_op jit(solution)/shard_map/ppermute | solution.py:291
  8.4 4.8 %collective-permute-done.5.refs_1_ = bf16[32,4480]{1,0:T(8,128)(2,1)S(1)} collective-permute-done((bf16[32,4480]{1,0:T(8,128)(2,1)S(1)}, bf16[32,4480]{1,0:T(8,128)(2,1)S(1)}, u32[]{:S(2)}, u32[]{:S(2)}) %collective-permute-start.5) | collective-permute-done | bytes 286752 | tf_op jit(solution)/shard_map/ppermute | solution.py:291
  13.2 7.4 %collective-permute-done.6.refs_2_ = bf16[32,4480]{1,0:T(8,128)(2,1)S(1)} collective-permute-done((bf16[32,4480]{1,0:T(8,128)(2,1)S(1)}, bf16[32,4480]{1,0:T(8,128)(2,1)S(1)}, u32[]{:S(2)}, u32[]{:S(2)}) %collective-permute-start.6) | collective-permute-done | bytes 286752 | tf_op jit(solution)/shard_map/ppermute | solution.py:291
  20.6 1.9 %copy-done = bf16[1,384,4096]{2,1,0:T(8,128)(2,1)S(1)} copy-done((bf16[1,384,4096]{2,1,0:T(8,128)(2,1)S(1)}, bf16[1,384,4096]{2,1,0:T(8,128)(2,1)}, u32[]{:S(2)}) %copy-start) | copy-done | bytes 3145752
  22.5 0.7 %copy-done.8 = f32[1,12,32]{2,0,1:T(1,128)S(1)} copy-done((f32[1,12,32]{2,0,1:T(1,128)S(1)}, f32[1,12,32]{2,0,1:T(1,128)}, u32[]{:S(2)}) %copy-start.8) | copy-done | bytes 1560
  23.2 3.8 %help_both.1 = (bf16[32,4480]{1,0:T(8,128)(2,1)S(1)}, bf16[32,4480]{1,0:T(8,128)(2,1)}, bf16[32,4480]{1,0:T(8,128)(2,1)}, bf16[32,4480]{1,0:T(8,128)(2,1)}, bf16...) custom-call(s32[1]{0:T(128)} %copy.17.hot_ref, f32[12,1,32]{2,1,0:T(1,128)S(1)} %bitcast.29, ...), custom_call_target="tpu_custom_call" | custom-call | flops 805306368 | bytes 5439488 | tf_op jit(solution)/shard_map/help_both/pallas_call | solution.py:271
  27.1 1.3 %collective-permute-start.10 = (bf16[32,4480]{1,0:T(8,128)(2,1)}, bf16[32,4480]{1,0:T(8,128)(2,1)}, u32[]{:S(2)}, u32[]{:S(2)}) collective-permute-start(bf16[32,4480]{1,0:T(8,128)(2,1)} %get-tuple-element.29), channel_id=1, source_target_pairs={{0,8},{4,12},{8,0},{12,4},{16,24},{20,28},{24,16},{28,20},{1,9},{5... | collective-permute-start | bytes 860168 | tf_op jit(solution)/shard_map/ppermute | solution.py:291
  28.3 1.8 %collective-permute-start.8 = (bf16[32,4480]{1,0:T(8,128)(2,1)}, bf16[32,4480]{1,0:T(8,128)(2,1)}, u32[]{:S(2)}, u32[]{:S(2)}) collective-permute-start(bf16[32,4480]{1,0:T(8,128)(2,1)} %get-tuple-element.27), channel_id=1, source_target_pairs={{0,24},{4,28},{8,16},{12,20},{16,8},{20,12},{24,0},{28,4},{1,25},{... | collective-permute-start | bytes 860168 | tf_op jit(solution)/shard_map/ppermute | solution.py:291
  30.1 0.5 collective-permute-start.9
  31.3 2.6 %own_forward.1 = (bf16[128,1024]{1,0:T(8,128)(2,1)S(1)}, bf16[128,1024]{1,0:T(8,128)(2,1)}, bf16[128,1024]{1,0:T(8,128)(2,1)S(1)}, bf16[128,1024]{1,0:T(8,128)(2,1)S(1)}) custom-call(f32[12,1,32]{2,1,0:T(1,128)S(1)} %bitcast.30, s32[1]{0:T(128)S(6)} %copy.15.count_ref, bf16[128,384]{1,0:T(8,128)(2,1)S(1)} %bitcast.26, bf16[384,4096]{1,0:T(8,128)(2,1)S(1)} %bitcast.23), custom_call_target="tpu_custom_call" | custom-call | flops 402653184 | bytes 4292608 | tf_op jit(solution)/shard_map/own_forward/pallas_call | solution.py:149
  33.8 0.7 %copy-done.4 = bf16[128,1024]{1,0:T(8,128)(2,1)} copy-done((bf16[128,1024]{1,0:T(8,128)(2,1)}, bf16[128,1024]{1,0:T(8,128)(2,1)S(1)}, u32[]{:S(2)}) %copy-start.4) | copy-done | bytes 262168
  34.5 0.7 %copy-done.10 = bf16[128,1024]{1,0:T(8,128)(2,1)} copy-done((bf16[128,1024]{1,0:T(8,128)(2,1)}, bf16[128,1024]{1,0:T(8,128)(2,1)S(1)}, u32[]{:S(2)}) %copy-start.10) | copy-done | bytes 262168
  35.3 0.7 %copy-done.12 = bf16[128,1024]{1,0:T(8,128)(2,1)} copy-done((bf16[128,1024]{1,0:T(8,128)(2,1)}, bf16[128,1024]{1,0:T(8,128)(2,1)S(1)}, u32[]{:S(2)}) %copy-start.12) | copy-done | bytes 262168
  36.0 1.6 %collective-permute-start = (bf16[128,1024]{1,0:T(8,128)(2,1)}, bf16[128,1024]{1,0:T(8,128)(2,1)}, u32[]{:S(2)}, u32[]{:S(2)}) collective-permute-start(bf16[128,1024]{1,0:T(8,128)(2,1)} %get-tuple-element.24), channel_id=1, source_target_pairs={{0,1},{1,0},{2,3},{3,2},{4,5},{5,4},{6,7},{7,6},{8,9},{9,8},{10,11... | collective-permute-start | bytes 786440 | tf_op jit(solution)/shard_map/ppermute | solution.py:291
  37.5 2.6 %collective-permute-start.1 = (bf16[128,1024]{1,0:T(8,128)(2,1)}, bf16[128,1024]{1,0:T(8,128)(2,1)S(1)}, u32[]{:S(2)}, u32[]{:S(2)}) collective-permute-start(bf16[128,1024]{1,0:T(8,128)(2,1)} %copy-done.12), channel_id=1, source_target_pairs={{0,2},{1,3},{2,0},{3,1},{4,6},{5,7},{6,4},{7,5},{8,10},{9,11},{10,... | collective-permute-start | bytes 786440 | tf_op jit(solution)/shard_map/ppermute | solution.py:291
  40.1 1.2 %copy-done.2 = bf16[1,128,4096]{2,1,0:T(8,128)(2,1)S(1)} copy-done((bf16[1,128,4096]{2,1,0:T(8,128)(2,1)S(1)}, bf16[1,128,4096]{2,1,0:T(8,128)(2,1)}, u32[]{:S(2)}) %copy-start.2) | copy-done | bytes 1048600
  41.4 0.9 %copy-done.7 = bf16[128,896]{1,0:T(8,128)(2,1)S(1)} copy-done((bf16[128,896]{1,0:T(8,128)(2,1)S(1)}, bf16[128,896]{1,0:T(8,128)(2,1)}, u32[]{:S(2)}) %copy-start.7) | copy-done | bytes 229400
  42.3 4.4 %own_backward.1 = (bf16[128,384]{1,0:T(8,128)(2,1)}, bf16[384,4096]{1,0:T(8,128)(2,1)}, f32[384,512]{1,0:T(8,128)}) custom-call(f32[12,1,32]{2,1,0:T(1,128)S(1)} %bitcast.31, s32[1]{0:T(128)S(6)} %copy.15.count_ref, bf16[128,384]{1,0:T(8,128)(2,1)S(1)} %bitcast.27, bf16[128,4096]{1,0:T(8,128)(2,1)S(1)} %bitcast.25, bf16[384,4096]{1,0:T(8,128)(2,1)S(1)} %bitcast.24, ...), custom_call_target="tpu_custom_call" | custom-call | flops 905969664 | bytes 9371648 | tf_op jit(solution)/shard_map/own_backward/pallas_call | solution.py:200
  46.7 0.3 collective-permute-start.2
  47.0 1.0 %select_select_fusion = bf16[32,4480]{1,0:T(8,128)(2,1)S(1)} fusion(bf16[32,4480]{1,0:T(8,128)(2,1)} %collective-permute-done.8, bf16[32,4480]{1,0:T(8,128)(2,1)} %collective-permute-done.9, bf16[32,4480]{1,0:T(8,128)(2,1)} %collective-permute-done.10, bf16[32,4480]{1,0:T(8,128)(2,1)S(1)} %get-tuple-element.30, pred[]{:T(512)S(6)} %eq.11, pred[]{:T(512)S(6)} %eq.10, ...), kind=kLoop, calls=%fused_computation.2 | loop fusion | flops 430080 | bytes 1433603 | tf_op jit(solution)/shard_map/jit(_where)/select_n | solution.py:308
  48.0 0.7 %collective-permute-start.12 = (bf16[32,1024]{1,0:T(8,128)(2,1)S(1)}, bf16[32,1024]{1,0:T(8,128)(2,1)S(1)}, u32[]{:S(2)}, u32[]{:S(2)}) collective-permute-start(bf16[32,1024]{1,0:T(8,128)(2,1)S(1)} %get-tuple-element.40), channel_id=1, source_target_pairs={{0,1},{1,0},{2,3},{3,2},{4,5},{5,4},{6,7},{7,6},{8,9},{9,8},{10,11... | collective-permute-start | bytes 196616 | tf_op jit(solution)/shard_map/ppermute | solution.py:291
  48.8 3.5 %collective-permute-start.13 = (bf16[32,1024]{1,0:T(8,128)(2,1)S(1)}, bf16[32,1024]{1,0:T(8,128)(2,1)S(1)}, u32[]{:S(2)}, u32[]{:S(2)}) collective-permute-start(bf16[32,1024]{1,0:T(8,128)(2,1)S(1)} %get-tuple-element.42), channel_id=1, source_target_pairs={{0,2},{1,3},{2,0},{3,1},{4,6},{5,7},{6,4},{7,5},{8,10},{9,11},{10,... | collective-permute-start | bytes 196616 | tf_op jit(solution)/shard_map/ppermute | solution.py:291
  52.5 4.0 %collective-permute-done.1 = bf16[128,1024]{1,0:T(8,128)(2,1)S(1)} collective-permute-done((bf16[128,1024]{1,0:T(8,128)(2,1)}, bf16[128,1024]{1,0:T(8,128)(2,1)S(1)}, u32[]{:S(2)}, u32[]{:S(2)}) %collective-permute-start.1) | collective-permute-done | bytes 262176 | tf_op jit(solution)/shard_map/ppermute | solution.py:291
  56.4 2.2 %collective-permute-done.2 = bf16[128,1024]{1,0:T(8,128)(2,1)S(1)} collective-permute-done((bf16[128,1024]{1,0:T(8,128)(2,1)S(1)}, bf16[128,1024]{1,0:T(8,128)(2,1)S(1)}, u32[]{:S(2)}, u32[]{:S(2)}) %collective-permute-start.2) | collective-permute-done | bytes 262176 | tf_op jit(solution)/shard_map/ppermute | solution.py:291
  58.6 1.8 %fusion = bf16[1,128,1024]{2,1,0:T(8,128)(2,1)} fusion(bf16[128,1024]{1,0:T(8,128)(2,1)S(1)} %collective-permute-done.2, bf16[128,1024]{1,0:T(8,128)(2,1)S(1)} %collective-permute-done.1, bf16[128,1024]{1,0:T(8,128)(2,1)} %collective-permute-done, bf16[128,1024]{1,0:T(8,128)(2,1)S(1)} %copy-done.5), kind=kLoop, calls=%fused_computation.3 | loop fusion | flops 1048576 | bytes 1310720 | tf_op jit(solution)/shard_map/broadcast_in_dim | solution.py:348
  60.5 0.6 slice_bitcast_fusion
  61.1 6.3 %collective-permute-done.13 = bf16[32,1024]{1,0:T(8,128)(2,1)S(1)} collective-permute-done((bf16[32,1024]{1,0:T(8,128)(2,1)S(1)}, bf16[32,1024]{1,0:T(8,128)(2,1)S(1)}, u32[]{:S(2)}, u32[]{:S(2)}) %collective-permute-start.13) | collective-permute-done | bytes 65568 | tf_op jit(solution)/shard_map/ppermute | solution.py:291
  67.4 0.7 fusion.1
  (34 shorter events, 0.3 us)
Async XLA Ops:
  0.6 20.0 %collective-permute-start.4 = (bf16[384,4096]{1,0:T(8,128)(2,1)}, bf16[384,4096]{1,0:T(8,128)(2,1)S(1)}, u32[]{:S(2)}, u32[]{:S(2)}) collective-permute-start(bf16[384,4096]{1,0:T(8,128)(2,1)} %bitcast.21), channel_id=1, source_target_pairs={{0,4},{4,0},{8,12},{12,8},{16,20},{20,16},{24,28},{28,24},{1,5},{5... | collective-permute-start | bytes 9437192 | tf_op jit(solution)/shard_map/ppermute | solution.py:291
  2.9 10.2 %collective-permute-start.5 = (bf16[32,4480]{1,0:T(8,128)(2,1)S(1)}, bf16[32,4480]{1,0:T(8,128)(2,1)S(1)}, u32[]{:S(2)}, u32[]{:S(2)}) collective-permute-start(bf16[32,4480]{1,0:T(8,128)(2,1)S(1)} %maximum_select_fusion.refs_0_), channel_id=1, source_target_pairs={{0,8},{4,12},{8,0},{12,4},{16,24},{20,28},{24,16},{28,20},{1,9},{5... | collective-permute-start | bytes 860168 | tf_op jit(solution)/shard_map/ppermute | solution.py:291
  5.5 15.1 %collective-permute-start.6 = (bf16[32,4480]{1,0:T(8,128)(2,1)S(1)}, bf16[32,4480]{1,0:T(8,128)(2,1)S(1)}, u32[]{:S(2)}, u32[]{:S(2)}) collective-permute-start(bf16[32,4480]{1,0:T(8,128)(2,1)S(1)} %maximum_select_fusion.refs_0_), channel_id=1, source_target_pairs={{0,16},{4,20},{8,24},{12,28},{16,0},{20,4},{24,8},{28,12},{1,17},{... | collective-permute-start | bytes 860168 | tf_op jit(solution)/shard_map/ppermute | solution.py:291
  7.0 13.6 %collective-permute-start.7 = (bf16[32,4480]{1,0:T(8,128)(2,1)S(1)}, bf16[32,4480]{1,0:T(8,128)(2,1)S(1)}, u32[]{:S(2)}, u32[]{:S(2)}) collective-permute-start(bf16[32,4480]{1,0:T(8,128)(2,1)S(1)} %maximum_select_fusion.refs_0_), channel_id=1, source_target_pairs={{0,24},{4,28},{8,16},{12,20},{16,8},{20,12},{24,0},{28,4},{1,25},{... | collective-permute-start | bytes 860168 | tf_op jit(solution)/shard_map/ppermute | solution.py:291
  7.0 1.4 %collective-permute-start.3 = (f32[12,1,32]{2,1,0:T(1,128)}, f32[12,1,32]{2,1,0:T(1,128)S(1)}, u32[]{:S(2)}, u32[]{:S(2)}) collective-permute-start(f32[12,1,32]{2,1,0:T(1,128)} %bitcast.28), channel_id=1, source_target_pairs={{0,4},{4,0},{8,12},{12,8},{16,20},{20,16},{24,28},{28,24},{1,5},{5... | collective-permute-start | bytes 4616 | tf_op jit(solution)/shard_map/ppermute | solution.py:291
  20.6 1.9 %copy-start = (bf16[1,384,4096]{2,1,0:T(8,128)(2,1)S(1)}, bf16[1,384,4096]{2,1,0:T(8,128)(2,1)}, u32[]{:S(2)}) copy-start(bf16[1,384,4096]{2,1,0:T(8,128)(2,1)} %param.9) | copy-start | bytes 9437188
  22.5 0.7 %copy-start.8 = (f32[1,12,32]{2,0,1:T(1,128)S(1)}, f32[1,12,32]{2,0,1:T(1,128)}, u32[]{:S(2)}) copy-start(f32[1,12,32]{2,0,1:T(1,128)} %param.10) | copy-start | bytes 4612
  23.2 8.1 %copy-start.1 = (bf16[1,384,4096]{2,1,0:T(8,128)(2,1)S(1)}, bf16[1,384,4096]{2,1,0:T(8,128)(2,1)}, u32[]{:S(2)}) copy-start(bf16[1,384,4096]{2,1,0:T(8,128)(2,1)} %param.9) | copy-start | bytes 9437188
  23.2 8.1 %copy-start.3 = (bf16[1,128,384]{2,1,0:T(8,128)(2,1)S(1)}, bf16[1,128,384]{2,1,0:T(8,128)(2,1)}, u32[]{:S(2)}) copy-start(bf16[1,128,384]{2,1,0:T(8,128)(2,1)} %param.11) | copy-start | bytes 294916
  27.0 6.8 %copy-start.6 = (bf16[128,896]{1,0:T(8,128)(2,1)}, bf16[128,896]{1,0:T(8,128)(2,1)S(1)}, u32[]{:S(2)}) copy-start(bf16[128,896]{1,0:T(8,128)(2,1)S(1)} %get-tuple-element.35.ours) | copy-start | bytes 688132
  27.0 13.1 %copy-start.9 = (f32[1,12,32]{2,0,1:T(1,128)S(1)}, f32[1,12,32]{2,0,1:T(1,128)}, u32[]{:S(2)}) copy-start(f32[1,12,32]{2,0,1:T(1,128)} %param.10) | copy-start | bytes 4612
  27.0 10.5 %collective-permute-start.11 = (bf16[128,896]{1,0:T(8,128)(2,1)}, bf16[128,896]{1,0:T(8,128)(2,1)}, u32[]{:S(2)}, u32[]{:S(2)}) collective-permute-start(bf16[128,896]{1,0:T(8,128)(2,1)} %get-tuple-element.36), channel_id=1, source_target_pairs={{0,4},{4,0},{8,12},{12,8},{16,20},{20,16},{24,28},{28,24},{1,5},{5... | collective-permute-start | bytes 688136 | tf_op jit(solution)/shard_map/ppermute | solution.py:291
  27.1 19.6 %collective-permute-start.10 = (bf16[32,4480]{1,0:T(8,128)(2,1)}, bf16[32,4480]{1,0:T(8,128)(2,1)}, u32[]{:S(2)}, u32[]{:S(2)}) collective-permute-start(bf16[32,4480]{1,0:T(8,128)(2,1)} %get-tuple-element.29), channel_id=1, source_target_pairs={{0,8},{4,12},{8,0},{12,4},{16,24},{20,28},{24,16},{28,20},{1,9},{5... | collective-permute-start | bytes 860168 | tf_op jit(solution)/shard_map/ppermute | solution.py:291
  28.3 18.6 %collective-permute-start.8 = (bf16[32,4480]{1,0:T(8,128)(2,1)}, bf16[32,4480]{1,0:T(8,128)(2,1)}, u32[]{:S(2)}, u32[]{:S(2)}) collective-permute-start(bf16[32,4480]{1,0:T(8,128)(2,1)} %get-tuple-element.27), channel_id=1, source_target_pairs={{0,24},{4,28},{8,16},{12,20},{16,8},{20,12},{24,0},{28,4},{1,25},{... | collective-permute-start | bytes 860168 | tf_op jit(solution)/shard_map/ppermute | solution.py:291
  30.1 16.9 %collective-permute-start.9 = (bf16[32,4480]{1,0:T(8,128)(2,1)}, bf16[32,4480]{1,0:T(8,128)(2,1)}, u32[]{:S(2)}, u32[]{:S(2)}) collective-permute-start(bf16[32,4480]{1,0:T(8,128)(2,1)} %get-tuple-element.28), channel_id=1, source_target_pairs={{0,16},{4,20},{8,24},{12,28},{16,0},{20,4},{24,8},{28,12},{1,17},{... | collective-permute-start | bytes 860168 | tf_op jit(solution)/shard_map/ppermute | solution.py:291
  33.8 0.7 %copy-start.4 = (bf16[128,1024]{1,0:T(8,128)(2,1)}, bf16[128,1024]{1,0:T(8,128)(2,1)S(1)}, u32[]{:S(2)}) copy-start(bf16[128,1024]{1,0:T(8,128)(2,1)S(1)} %get-tuple-element.31) | copy-start | bytes 786436
  34.5 0.7 %copy-start.10 = (bf16[128,1024]{1,0:T(8,128)(2,1)}, bf16[128,1024]{1,0:T(8,128)(2,1)S(1)}, u32[]{:S(2)}) copy-start(bf16[128,1024]{1,0:T(8,128)(2,1)S(1)} %get-tuple-element.26) | copy-start | bytes 786436
  35.2 0.7 %copy-start.12 = (bf16[128,1024]{1,0:T(8,128)(2,1)}, bf16[128,1024]{1,0:T(8,128)(2,1)S(1)}, u32[]{:S(2)}) copy-start(bf16[128,1024]{1,0:T(8,128)(2,1)S(1)} %get-tuple-element.25) | copy-start | bytes 786436
  36.0 16.3 %collective-permute-start = (bf16[128,1024]{1,0:T(8,128)(2,1)}, bf16[128,1024]{1,0:T(8,128)(2,1)}, u32[]{:S(2)}, u32[]{:S(2)}) collective-permute-start(bf16[128,1024]{1,0:T(8,128)(2,1)} %get-tuple-element.24), channel_id=1, source_target_pairs={{0,1},{1,0},{2,3},{3,2},{4,5},{5,4},{6,7},{7,6},{8,9},{9,8},{10,11... | collective-permute-start | bytes 786440 | tf_op jit(solution)/shard_map/ppermute | solution.py:291
  37.5 18.9 %collective-permute-start.1 = (bf16[128,1024]{1,0:T(8,128)(2,1)}, bf16[128,1024]{1,0:T(8,128)(2,1)S(1)}, u32[]{:S(2)}, u32[]{:S(2)}) collective-permute-start(bf16[128,1024]{1,0:T(8,128)(2,1)} %copy-done.12), channel_id=1, source_target_pairs={{0,2},{1,3},{2,0},{3,1},{4,6},{5,7},{6,4},{7,5},{8,10},{9,11},{10,... | collective-permute-start | bytes 786440 | tf_op jit(solution)/shard_map/ppermute | solution.py:291
  40.1 1.2 %copy-start.2 = (bf16[1,128,4096]{2,1,0:T(8,128)(2,1)S(1)}, bf16[1,128,4096]{2,1,0:T(8,128)(2,1)}, u32[]{:S(2)}) copy-start(bf16[1,128,4096]{2,1,0:T(8,128)(2,1)} %param.12) | copy-start | bytes 3145732
  41.4 0.9 %copy-start.7 = (bf16[128,896]{1,0:T(8,128)(2,1)S(1)}, bf16[128,896]{1,0:T(8,128)(2,1)}, u32[]{:S(2)}) copy-start(bf16[128,896]{1,0:T(8,128)(2,1)} %copy-done.6) | copy-start | bytes 688132
  42.3 4.4 %copy-start.11 = (bf16[128,1024]{1,0:T(8,128)(2,1)S(1)}, bf16[128,1024]{1,0:T(8,128)(2,1)}, u32[]{:S(2)}) copy-start(bf16[128,1024]{1,0:T(8,128)(2,1)} %copy-done.10) | copy-start | bytes 786436
  42.3 16.4 %copy-start.5 = (bf16[128,1024]{1,0:T(8,128)(2,1)S(1)}, bf16[128,1024]{1,0:T(8,128)(2,1)}, u32[]{:S(2)}) copy-start(bf16[128,1024]{1,0:T(8,128)(2,1)} %copy-done.4) | copy-start | bytes 786436
  46.7 12.0 %collective-permute-start.2 = (bf16[128,1024]{1,0:T(8,128)(2,1)S(1)}, bf16[128,1024]{1,0:T(8,128)(2,1)S(1)}, u32[]{:S(2)}, u32[]{:S(2)}) collective-permute-start(bf16[128,1024]{1,0:T(8,128)(2,1)S(1)} %copy-done.11), channel_id=1, source_target_pairs={{0,3},{1,2},{2,1},{3,0},{4,7},{5,6},{6,5},{7,4},{8,11},{9,10},{10,... | collective-permute-start | bytes 786440 | tf_op jit(solution)/shard_map/ppermute | solution.py:291
  48.0 13.0 %collective-permute-start.12 = (bf16[32,1024]{1,0:T(8,128)(2,1)S(1)}, bf16[32,1024]{1,0:T(8,128)(2,1)S(1)}, u32[]{:S(2)}, u32[]{:S(2)}) collective-permute-start(bf16[32,1024]{1,0:T(8,128)(2,1)S(1)} %get-tuple-element.40), channel_id=1, source_target_pairs={{0,1},{1,0},{2,3},{3,2},{4,5},{5,4},{6,7},{7,6},{8,9},{9,8},{10,11... | collective-permute-start | bytes 196616 | tf_op jit(solution)/shard_map/ppermute | solution.py:291
  48.8 18.6 %collective-permute-start.13 = (bf16[32,1024]{1,0:T(8,128)(2,1)S(1)}, bf16[32,1024]{1,0:T(8,128)(2,1)S(1)}, u32[]{:S(2)}, u32[]{:S(2)}) collective-permute-start(bf16[32,1024]{1,0:T(8,128)(2,1)S(1)} %get-tuple-element.42), channel_id=1, source_target_pairs={{0,2},{1,3},{2,0},{3,1},{4,6},{5,7},{6,4},{7,5},{8,10},{9,11},{10,... | collective-permute-start | bytes 196616 | tf_op jit(solution)/shard_map/ppermute | solution.py:291
  52.3 15.1 %collective-permute-start.14 = (bf16[32,1024]{1,0:T(8,128)(2,1)S(1)}, bf16[32,1024]{1,0:T(8,128)(2,1)S(1)}, u32[]{:S(2)}, u32[]{:S(2)}) collective-permute-start(bf16[32,1024]{1,0:T(8,128)(2,1)S(1)} %get-tuple-element.41), channel_id=1, source_target_pairs={{0,3},{1,2},{2,1},{3,0},{4,7},{5,6},{6,5},{7,4},{8,11},{9,10},{10,... | collective-permute-start | bytes 196616 | tf_op jit(solution)/shard_map/ppermute | solution.py:291
